TPU v7x, 32 devices: a whole 2x2x4 slice. The times are simulated.
32 devices in a mesh: dp: 8 (over y, x, core), vocab: 4 (over z).
Axes of the slice: x: 2, y: 2, z: 4, core: 2. Of those that a mesh axis runs over, the one named last changes fastest.
Arguments:
- hidden: bfloat16 [64, 4096], P('dp'), may hold values from -16 to 16
- embed_grad: bfloat16 [64, 4096], P('dp'), may hold values from -3 to 3
- token_ids: int32 [64], P('dp'), may hold values from 0 to 32767
- loss_weight: float32 [64], P('dp'), may hold values from 16 to 256
- teacher_logits: bfloat16 [64, 32768], P('dp', 'vocab'), may hold values from -24 to 256
- head: bfloat16 [4096, 32768], P('dp', 'vocab'), may hold values from -1 to 1
Outputs:
- grad_hidden: bfloat16 [64, 4096], P('dp', 'vocab')
- head_grad: float32 [4096, 32768], P('dp', 'vocab')
Inputs may be any that keep to these rules, and one draw needn't show every extreme that they name: `token_ids`: token ids of the vocabulary window.
All inputs are finite; a program needn't handle non-finite values.
Results may differ from a plain program's by a relative error of at most 0.0022.
The roundings to bfloat16 on the way count: a program that leaves them out, or rounds other values in their place, can miss the bound.
Values may be sent and summed in bfloat16 or wider, within the bound.
A program may use at most 128 MiB of HBM per device.

v0:
```python
import jax
import jax.numpy as jnp
from jax import lax
from jax.sharding import PartitionSpec as P


def combined_all(part, axis, combine):
    gathered = jax.tree.map(lambda a: lax.all_gather(a, axis), part)

    def take(source):
        return jax.tree.map(lambda a: lax.dynamic_index_in_dim(a, source, 0, False), gathered)

    return lax.fori_loop(
        1, lax.axis_size(axis), lambda source, state: combine(state, take(source)), take(0)
    )


def contract_rows(left, right):
    return lax.dot_general(
        left, right, (((0,), (0,)), ((), ())), preferred_element_type=jnp.float32
    )


def contract_cols(left, right):
    return lax.dot_general(
        left, right, (((1,), (1,)), ((), ())), preferred_element_type=jnp.float32
    )


def combine_pairs(earlier, later):
    s_max_a, s_sum_a, t_max_a, t_sum_a = earlier
    s_max_b, s_sum_b, t_max_b, t_sum_b = later
    s_max = jnp.maximum(s_max_a, s_max_b)
    t_max = jnp.maximum(t_max_a, t_max_b)
    s_sum = s_sum_a * jnp.exp(s_max_a - s_max) + s_sum_b * jnp.exp(s_max_b - s_max)
    t_sum = t_sum_a * jnp.exp(t_max_a - t_max) + t_sum_b * jnp.exp(t_max_b - t_max)
    return (s_max, s_sum, t_max, t_sum)


def per_device(hidden, embed_grad, token_ids, loss_weight, teacher_logits, head):
    vocab_width = head.shape[1]
    hidden_cols, embed_cols = (
        lax.all_to_all(hidden, "dp", split_axis=1, concat_axis=0, tiled=True),
        lax.all_to_all(embed_grad, "dp", split_axis=1, concat_axis=0, tiled=True),
    )
    student = lax.psum_scatter(
        jnp.dot(hidden_cols, head, preferred_element_type=jnp.float32),
        "dp",
        scatter_dimension=0,
        tiled=True,
    )
    teacher = teacher_logits.astype(jnp.float32)
    student_max = jnp.max(student, axis=1)
    teacher_max = jnp.max(teacher, axis=1)
    student_sum = jnp.sum(jnp.exp(student - student_max[:, None]), axis=1)
    teacher_sum = jnp.sum(jnp.exp(teacher - teacher_max[:, None]), axis=1)
    student_top, student_total, teacher_top, teacher_total = combined_all(
        (student_max, student_sum, teacher_max, teacher_sum), "vocab", combine_pairs
    )
    student_norm = student_top + jnp.log(student_total)
    teacher_norm = teacher_top + jnp.log(teacher_total)
    gap = (
        loss_weight[:, None]
        * (jnp.exp(student - student_norm[:, None]) - jnp.exp(teacher - teacher_norm[:, None]))
    ).astype(jnp.bfloat16)
    vocab_ids = lax.axis_index("vocab") * vocab_width + jnp.arange(vocab_width, dtype=jnp.int32)
    gap_piece = lax.all_gather(gap, "dp", axis=0, tiled=True)
    id_piece = lax.all_gather(token_ids, "dp", axis=0, tiled=True)
    lookup = (id_piece[:, None] == vocab_ids[None, :]).astype(jnp.bfloat16)
    grad_rows = contract_rows(hidden_cols, gap_piece) + contract_rows(embed_cols, lookup)
    back_cols = contract_cols(gap_piece, head)
    head_grad, back_cols = (grad_rows, back_cols)
    regrouped = lax.all_to_all(back_cols, "dp", split_axis=0, concat_axis=1, tiled=True)
    grad_hidden = lax.psum_scatter(regrouped, "vocab", scatter_dimension=1, tiled=True).astype(
        jnp.bfloat16
    )
    return (grad_hidden, head_grad)


def solution(mesh):
    placed = (P("dp", None), P("dp", None), P("dp"), P("dp"), P("dp", "vocab"), P("dp", "vocab"))
    return jax.shard_map(
        per_device,
        mesh=mesh,
        in_specs=placed,
        out_specs=(P("dp", "vocab"), P("dp", "vocab")),
        check_vma=False,
    )
```

profile of v0, /device:TPU:0, one launch (start us, length us, event | category | flops | bytes accessed | tf_op | source)
XLA Modules:
  0.0 173.7 jit_solution(2264943251010884728)
XLA Ops:
  7.2 0.0 reduce-scatter.3.cloned.1.call-start
  7.2 10.2 %all_to_all.57 = bf16[8,8,512]{2,0,1:T(8,128)(2,1)S(1)} all-to-all(bf16[8,8,512]{2,0,1:T(8,128)(2,1)} %bitcast.60), channel_id=1, replica_groups=mesh['dp'=8,'vocab'=4] {'dp'}, dimensions={1} | all-to-all | bytes 131072 | tf_op jit(solution)/shard_map/all_to_all | solution.py:43
  17.4 0.0 copy-start.1
  17.4 0.0 copy-start.6
  17.4 6.3 %fusion.22 = f32[64,8192]{1,0:T(8,128)} fusion(bf16[512,8192]{1,0:T(8,128)(2,1)} %param.13, bf16[8,8,512]{2,0,1:T(8,128)(2,1)S(1)} %all_to_all.57), kind=kOutput, calls=%fused_computation.31 | convolution fusion | flops 536870912 | bytes 10551296 | tf_op jit(solution)/shard_map/dot_general | solution.py:47
  23.8 0.0 reduce-scatter.3.cloned.1.call-update
  23.8 0.0 all-gather.6.cloned.1.call-start
  23.8 0.0 copy-done.1
  23.8 0.2 reduce_max.28
  24.0 0.0 copy-done.6
  24.0 0.6 dynamic-slice
  25.3 0.3 fusion.14
  25.6 0.2 dynamic-update-slice.3
  25.8 0.1 convert_dynamic-update-slice_fusion
  25.9 38.6 %reduce-scatter.3.cloned.1.call-done = f32[8,8192]{1,0:T(8,128)} async-done(((f32[64,8192]{1,0:T(8,128)}), f32[8,8192]{1,0:T(8,128)}) %reduce-scatter.3.cloned.1.call-update) | async-done | bytes 262160 | tf_op jit(solution)/shard_map/reduce_scatter | solution.py:46
  64.5 1.1 reduce_max.27
  65.6 0.2 dynamic-update-slice
  65.8 1.2 exponential_reduce_fusion
  67.0 0.2 dynamic-update-slice.1
  67.3 11.7 %all-reduce.5 = (f32[32]{0:T(128)S(1)}, f32[32]{0:T(128)S(1)}, f32[32]{0:T(128)S(1)}, f32[32]{0:T(128)S(1)}) all-reduce(f32[32]{0:T(128)S(1)} %dynamic-update-slice, f32[32]{0:T(128)S(1)} %dynamic-update-slice.1, f32[32]{0:T(128)S(1)} %convert_dynamic-update-slice_fusion, ...), channel_id=2, replica_groups=mesh['dp'=8,'vocab'=4] {'vocab'}, use_global_device_ids=true, to_apply=%add | all-reduce | flops 128 | bytes 1024
  78.9 0.1 reshape.35
  79.0 0.1 reshape.36
  79.1 0.1 reshape.37
  79.2 0.1 reshape.38
  79.3 0.1 while.21
  79.4 0.0 copy-done.3
  79.4 1.8 %fusion.18 = bf16[8,8192]{1,0:T(8,128)(2,1)} fusion(bf16[8,8192]{1,0:T(8,128)(2,1)S(1)} %copy-done.1, f32[8,8192]{1,0:T(8,128)} %reduce-scatter.3.cloned.1.call-done, f32[8]{0:T(128)S(1)} %get-tuple-element.259, f32[8]{0:T(128)S(1)} %get-tuple-element.260, f32[8]{0:T(128)S(1)} %copy-done.3), kind=kLoop, calls=%fused_computation.26 | loop fusion | flops 393216 | bytes 524384 | tf_op jit(solution)/shard_map/convert_element_type | solution.py:65
  81.2 0.0 all-gather.6.cloned.1.call-update
  81.2 20.8 %all-gather.6.cloned.1.call-done = bf16[64,8192]{1,0:T(8,128)(2,1)} async-done(((bf16[8,8192]{1,0:T(8,128)(2,1)}), bf16[64,8192]{1,0:T(8,128)(2,1)}) %all-gather.6.cloned.1.call-update) | async-done | bytes 1048592 | tf_op jit(solution)/shard_map/all_gather | solution.py:67
  102.0 7.1 %convolution_bitcast_fusion = f32[8,8,512]{2,1,0:T(8,128)} fusion(bf16[64,8192]{1,0:T(8,128)(2,1)} %all-gather.6.cloned.1.call-done, bf16[512,8192]{1,0:T(8,128)(2,1)} %param.13), kind=kOutput, calls=%fused_computation.16 | convolution fusion | flops 536870912 | bytes 9568256 | tf_op jit(solution)/shard_map/dot_general | solution.py:25
  109.1 3.4 %all-to-all-start.1 = ((f32[8,8,512]{2,1,0:T(8,128)}), f32[8,8,512]{2,1,0:T(8,128)S(1)}, u32[]{:S(2)}, u32[]{:S(2)}) async-start(f32[8,8,512]{2,1,0:T(8,128)} %convolution_bitcast_fusion), calls=%async_computation.2 | async-start | bytes 262144 | tf_op jit(solution)/shard_map/all_to_all | solution.py:73
  112.5 0.0 copy-done.5
  112.5 0.6 dynamic-slice.4
  113.7 0.0 copy-done.4
  113.7 0.2 dynamic-update-slice.4
  114.0 8.4 %all-reduce.4 = s32[64]{0:T(128)S(1)} all-reduce(s32[64]{0:T(128)S(1)} %dynamic-update-slice.4), channel_id=1, replica_groups=mesh['dp'=8,'vocab'=4] {'dp'}, use_global_device_ids=true, to_apply=%add.4 | all-reduce | flops 64 | bytes 512
  122.4 0.0 all-to-all-done.1
  122.4 0.0 copy-start.2
  122.4 3.4 %all-to-all-start.2 = ((bf16[8,8,512]{2,0,1:T(8,128)(2,1)}), bf16[8,8,512]{2,0,1:T(8,128)(2,1)S(1)}, u32[]{:S(2)}, u32[]{:S(2)}) async-start(bf16[8,8,512]{2,0,1:T(8,128)(2,1)} %bitcast.13), calls=%async_computation.4 | async-start | bytes 131072 | tf_op jit(solution)/shard_map/all_to_all | solution.py:44
  125.8 0.0 reduce-scatter.5.cloned.1.call-start
  125.8 0.0 copy-done
  125.8 8.5 %fusion.20 = f32[8192,512]{1,0:T(8,128)} fusion(bf16[64,8192]{1,0:T(8,128)(2,1)S(1)} %copy-done, bf16[8,8,512]{2,0,1:T(8,128)(2,1)S(1)} %all_to_all.57), kind=kOutput, calls=%fused_computation.29 | convolution fusion | flops 536870912 | bytes 17891328 | tf_op jit(solution)/shard_map/dot_general | solution.py:19
  134.4 0.0 copy-done.2
  134.4 0.0 reduce-scatter.5.cloned.1.call-update
  134.4 0.0 all-to-all-done.2
  134.4 13.9 %add_bitcast_fusion = f32[512,8192]{0,1:T(8,128)} fusion(f32[8192,512]{1,0:T(8,128)} %fusion.20, s32[8192]{0:T(1024)S(1)} %iota_add_fusion, s32[64]{0:T(128)S(1)} %all-reduce.4, bf16[8,8,512]{2,0,1:T(8,128)(2,1)S(1)} %all-to-all-done.2), kind=kOutput, calls=%fused_computation.14 | convolution fusion | flops 541589504 | bytes 33652992 | tf_op jit(solution)/shard_map/dot_general | solution.py:19
  148.4 17.4 %copy.8 = f32[512,8192]{1,0:T(8,128)} copy(f32[512,8192]{0,1:T(8,128)} %add_bitcast_fusion) | data formatting | bytes 33554432
  165.8 1.4 convert_element_type.12
  (16 shorter events, 0.1 us)
Async XLA Ops:
  7.2 57.3 %reduce-scatter.3.cloned.1.call-start = ((), (), s32[]{:S(2)}) async-start(), calls=%async_computation.5 | async-start | bytes 2359296 | tf_op jit(solution)/shard_map/reduce_scatter | solution.py:46
  17.4 6.4 %copy-start.1 = (bf16[8,8192]{1,0:T(8,128)(2,1)S(1)}, bf16[8,8192]{1,0:T(8,128)(2,1)}, u32[]{:S(2)}) copy-start(bf16[8,8192]{1,0:T(8,128)(2,1)} %param.12) | copy-start | bytes 393220
  17.4 6.6 %copy-start.6 = (u32[32]{0:T(128)S(1)}, u32[32]{0:T(128)}, u32[]{:S(2)}) copy-start(u32[32]{0:T(128)} %constant.69) | copy-start | bytes 388
  17.4 62.0 %copy-start.3 = (f32[8]{0:T(128)S(1)}, f32[8]{0:T(128)}, u32[]{:S(2)}) copy-start(f32[8]{0:T(128)} %param.11) | copy-start | bytes 100
  23.7 88.7 %copy-start.5 = (u32[32]{0:T(128)S(1)}, u32[32]{0:T(128)}, u32[]{:S(2)}) copy-start(u32[32]{0:T(128)} %constant.89) | copy-start | bytes 388
  23.7 90.0 %copy-start.4 = (s32[8]{0:T(128)S(1)}, s32[8]{0:T(128)}, u32[]{:S(2)}) copy-start(s32[8]{0:T(128)} %param.10) | copy-start | bytes 100
  23.8 78.2 %all-gather.6.cloned.1.call-start = ((), (), s32[]{:S(2)}) async-start(), calls=%async_computation.6 | async-start | bytes 1179648 | tf_op jit(solution)/shard_map/all_gather | solution.py:67
  102.0 23.9 %copy-start = (bf16[64,8192]{1,0:T(8,128)(2,1)S(1)}, bf16[64,8192]{1,0:T(8,128)(2,1)}, u32[]{:S(2)}) copy-start(bf16[64,8192]{1,0:T(8,128)(2,1)} %all-gather.6.cloned.1.call-done) | copy-start | bytes 3145732
  109.1 13.3 %all-to-all-start.1 = ((f32[8,8,512]{2,1,0:T(8,128)}), f32[8,8,512]{2,1,0:T(8,128)S(1)}, u32[]{:S(2)}, u32[]{:S(2)}) async-start(f32[8,8,512]{2,1,0:T(8,128)} %convolution_bitcast_fusion), calls=%async_computation.2 | async-start | bytes 262144 | tf_op jit(solution)/shard_map/all_to_all | solution.py:73
  122.4 12.0 %copy-start.2 = (f32[8,8,512]{2,1,0:T(8,128)}, f32[8,8,512]{2,1,0:T(8,128)S(1)}, u32[]{:S(2)}) copy-start(f32[8,8,512]{2,1,0:T(8,128)S(1)} %all-to-all-done.1) | copy-start | bytes 393220
  122.4 12.0 %all-to-all-start.2 = ((bf16[8,8,512]{2,0,1:T(8,128)(2,1)}), bf16[8,8,512]{2,0,1:T(8,128)(2,1)S(1)}, u32[]{:S(2)}, u32[]{:S(2)}) async-start(bf16[8,8,512]{2,0,1:T(8,128)(2,1)} %bitcast.13), calls=%async_computation.4 | async-start | bytes 131072 | tf_op jit(solution)/shard_map/all_to_all | solution.py:44
  125.8 40.0 %reduce-scatter.5.cloned.1.call-start = ((), (), s32[]{:S(2)}) async-start(), calls=%async_computation.7 | async-start | bytes 163840 | tf_op jit(solution)/shard_map/reduce_scatter | solution.py:74
Sparse Core Ops, SparseCore 0:
  23.9 40.5 reduce-scatter.2
  81.3 20.5 all-gather.5
  134.5 20.7 reduce-scatter.4
where the time goes:
time: 175 us; the launch traced here: 174 us
  waiting for transfers between devices  59.4 us (34%)
  matrix products  35.9 us (21%)
  blocking collectives  30.3 us (17%)
  local copies, waits for them, and re-layouts  20 us (11%)
  between operations  15.2 us (9%)
  starting transfers between devices  6.86 us (4%)
  other arithmetic  6.1 us (3%)
    reduce_scatter x1, waiting for transfers between devices, per_device(): lax.psum_scatter(jnp.dot(hidden_cols, head, preferred_element_type=jnp.fl...  38.6 us
    dot_general x2, matrix products, contract_rows(): lax.dot_general(left, right, (((0,), (0,)), ((), ())), preferred_element_...  22.5 us
    all_gather x1, waiting for transfers between devices, per_device(): gap_piece = lax.all_gather(gap, 'dp', axis=0, tiled=True)  20.8 us
    unnamed x2, blocking collectives  20.1 us
    unnamed x26, local copies, waits for them, and re-layouts  19.6 us
    all_to_all x1, blocking collectives, per_device(): lax.all_to_all(hidden, 'dp', split_axis=1, concat_axis=0, tiled=True)  10.2 us
    dot_general x1, matrix products, contract_cols(): lax.dot_general(left, right, (((1,), (1,)), ((), ())), preferred_element_...  7.1 us
    dot_general x1, matrix products, per_device(): jnp.dot(hidden_cols, head, preferred_element_type=jnp.float32)  6.31 us
  transfers between devices with their start and end apart: 5, of which 2 were waited for; matrix products, arithmetic and copies ran while one was open for 24% of the time, Pallas kernels for 0%

commit v1 on v0

--- a/solution.py
+++ b/solution.py
@@ -2,6 +2,7 @@
 import jax.numpy as jnp
 from jax import lax
 from jax.sharding import PartitionSpec as P
+from jax.lax import all_to_all, axis_size
 
 
 def combined_all(part, axis, combine):
@@ -39,8 +40,16 @@
 
 def per_device(hidden, embed_grad, token_ids, loss_weight, teacher_logits, head):
     vocab_width = head.shape[1]
+
+    def balance_sheet(chunk, lane_axis="dp"):
+        far_arr = axis_size(lane_axis)
+        known = jnp.split(chunk, far_arr, 1)
+        extra = jnp.stack(known)
+        r_now = all_to_all(extra, lane_axis, 0, 0)
+        return jnp.concatenate(r_now, 0)
+
     hidden_cols, embed_cols = (
-        lax.all_to_all(hidden, "dp", split_axis=1, concat_axis=0, tiled=True),
+        balance_sheet(hidden),
         lax.all_to_all(embed_grad, "dp", split_axis=1, concat_axis=0, tiled=True),
     )
     student = lax.psum_scatter(

time: 175 us -> 157 us (0.90)
  local copies, waits for them, and re-layouts: 20 us -> 8.75 us
  waiting for transfers between devices: 59.4 us -> 52.7 us
    all_gather x1, waiting for transfers between devices: 20.8 us -> 7.45 us  [per_device(): gap_piece = lax.all_gather(gap, 'dp', axis=0, tiled=True)]
    unnamed x26 -> x32, local copies, waits for them, and re-layouts: 19.6 us -> 7.72 us
    reduce_scatter x1, waiting for transfers between devices: 0.01 us -> 6.6 us  [per_device(): lax.psum_scatter(regrouped, 'vocab', scatter_dimension=1, tiled=True)]
  transfers between devices with their start and end apart: 5 -> 5, of which waited for: 2 -> 3; matrix products, arithmetic and copies ran while one was open for 24% -> 21% of each run, Pallas kernels for 0% -> 0%
where the time goes in v1:
time: 157 us; the launch traced here: 156 us
  waiting for transfers between devices  52.7 us (34%)
  matrix products  36.2 us (23%)
  blocking collectives  30.1 us (19%)
  between operations  15.2 us (10%)
  local copies, waits for them, and re-layouts  8.75 us (6%)
  starting transfers between devices  6.86 us (4%)
  other arithmetic  6.1 us (4%)
    reduce_scatter x1, waiting for transfers between devices, per_device(): lax.psum_scatter(jnp.dot(hidden_cols, head, preferred_element_type=jnp.fl...  38.6 us
    dot_general x2, matrix products, contract_rows(): lax.dot_general(left, right, (((0,), (0,)), ((), ())), preferred_element_...  22.9 us
    unnamed x2, blocking collectives  20.1 us
    all_to_all x1, blocking collectives, balance_sheet(): r_now = all_to_all(extra, lane_axis, 0, 0)  10 us
    unnamed x32, local copies, waits for them, and re-layouts  7.72 us
    all_gather x1, waiting for transfers between devices, per_device(): gap_piece = lax.all_gather(gap, 'dp', axis=0, tiled=True)  7.45 us
    dot_general x1, matrix products, contract_cols(): lax.dot_general(left, right, (((1,), (1,)), ((), ())), preferred_element_...  7.03 us
    reduce_scatter x1, waiting for transfers between devices, per_device(): lax.psum_scatter(regrouped, 'vocab', scatter_dimension=1, tiled=True)  6.6 us
  transfers between devices with their start and end apart: 5, of which 3 were waited for; matrix products, arithmetic and copies ran while one was open for 21% of the time, Pallas kernels for 0%

profile of v1, /device:TPU:0, one launch (start us, length us, event | category | flops | bytes accessed | tf_op | source)
XLA Modules:
  0.0 155.9 jit_solution(14438258762942651453)
XLA Ops:
  7.2 0.0 reduce-scatter.3.cloned.1.call-start
  7.2 0.7 constant_dynamic-update-slice_fusion.7
  7.9 0.7 constant_dynamic-update-slice_fusion.6
  8.6 0.7 constant_dynamic-update-slice_fusion.5
  9.3 0.7 constant_dynamic-update-slice_fusion.4
  10.0 0.7 constant_dynamic-update-slice_fusion.3
  10.7 0.7 constant_dynamic-update-slice_fusion.2
  11.4 0.7 constant_dynamic-update-slice_fusion.1
  12.1 0.7 constant_dynamic-update-slice_fusion
  12.8 10.0 %all_to_all.43 = bf16[8,8,512]{2,1,0:T(8,128)(2,1)S(1)} all-to-all(bf16[8,8,512]{2,1,0:T(8,128)(2,1)S(1)} %constant_dynamic-update-slice_fusion), channel_id=1, replica_groups=mesh['dp'=8,'vocab'=4] {'dp'}, dimensions={0} | all-to-all | bytes 131072 | tf_op jit(solution)/shard_map/all_to_all | solution.py:48
  22.8 0.0 copy-start.4
  22.8 6.3 %fusion.22 = f32[64,8192]{1,0:T(8,128)} fusion(bf16[512,8192]{1,0:T(8,128)(2,1)} %param.13, bf16[8,8,512]{2,1,0:T(8,128)(2,1)S(1)} %all_to_all.43), kind=kOutput, calls=%fused_computation.31 | convolution fusion | flops 536870912 | bytes 10551296 | tf_op jit(solution)/shard_map/dot_general | solution.py:56
  29.1 0.0 reduce-scatter.3.cloned.1.call-update
  29.2 0.0 all-gather.6.cloned.1.call-start
  29.2 0.2 reduce_max.28
  29.4 0.6 dynamic-slice
  30.7 0.3 fusion.15
  30.9 0.2 dynamic-update-slice.3
  31.2 0.1 convert_dynamic-update-slice_fusion
  31.3 38.6 %reduce-scatter.3.cloned.1.call-done = f32[8,8192]{1,0:T(8,128)} async-done(((f32[64,8192]{1,0:T(8,128)}), f32[8,8192]{1,0:T(8,128)}) %reduce-scatter.3.cloned.1.call-update) | async-done | bytes 262160 | tf_op jit(solution)/shard_map/reduce_scatter | solution.py:55
  69.8 1.1 reduce_max.27
  71.0 0.2 dynamic-update-slice
  71.2 1.2 exponential_reduce_fusion
  72.4 0.2 dynamic-update-slice.1
  72.7 11.7 %all-reduce.5 = (f32[32]{0:T(128)S(1)}, f32[32]{0:T(128)S(1)}, f32[32]{0:T(128)S(1)}, f32[32]{0:T(128)S(1)}) all-reduce(f32[32]{0:T(128)S(1)} %dynamic-update-slice, f32[32]{0:T(128)S(1)} %dynamic-update-slice.1, f32[32]{0:T(128)S(1)} %convert_dynamic-update-slice_fusion, ...), channel_id=2, replica_groups=mesh['dp'=8,'vocab'=4] {'vocab'}, use_global_device_ids=true, to_apply=%add | all-reduce | flops 128 | bytes 1024
  84.3 0.1 reshape.36
  84.4 0.1 reshape.37
  84.5 0.1 reshape.38
  84.6 0.1 reshape.39
  84.7 0.1 while.21
  84.8 1.8 %fusion.19 = bf16[8,8192]{1,0:T(8,128)(2,1)} fusion(bf16[8,8192]{1,0:T(8,128)(2,1)S(1)} %copy-done.1, f32[8,8192]{1,0:T(8,128)} %reduce-scatter.3.cloned.1.call-done, f32[8]{0:T(128)S(1)} %get-tuple-element.257, f32[8]{0:T(128)S(1)} %get-tuple-element.258, f32[8]{0:T(128)S(1)} %copy-done.3), kind=kLoop, calls=%fused_computation.27 | loop fusion | flops 393216 | bytes 524384 | tf_op jit(solution)/shard_map/convert_element_type | solution.py:74
  86.6 0.0 all-gather.6.cloned.1.call-update
  86.6 3.4 %all-to-all-start.2 = ((bf16[8,8,512]{2,0,1:T(8,128)(2,1)}), bf16[8,8,512]{2,0,1:T(8,128)(2,1)S(1)}, u32[]{:S(2)}, u32[]{:S(2)}) async-start(bf16[8,8,512]{2,0,1:T(8,128)(2,1)} %bitcast.18), calls=%async_computation.4 | async-start | bytes 131072 | tf_op jit(solution)/shard_map/all_to_all | solution.py:53
  90.0 0.6 dynamic-slice.4
  91.2 0.2 dynamic-update-slice.4
  91.5 8.4 %all-reduce.4 = s32[64]{0:T(128)S(1)} all-reduce(s32[64]{0:T(128)S(1)} %dynamic-update-slice.4), channel_id=1, replica_groups=mesh['dp'=8,'vocab'=4] {'dp'}, use_global_device_ids=true, to_apply=%add.4 | all-reduce | flops 64 | bytes 512
  99.9 7.5 %all-gather.6.cloned.1.call-done = bf16[64,8192]{1,0:T(8,128)(2,1)} async-done(((bf16[8,8192]{1,0:T(8,128)(2,1)}), bf16[64,8192]{1,0:T(8,128)(2,1)}) %all-gather.6.cloned.1.call-update) | async-done | bytes 1048592 | tf_op jit(solution)/shard_map/all_gather | solution.py:76
  107.4 7.0 %convolution_bitcast_fusion = f32[8,8,512]{2,1,0:T(8,128)} fusion(bf16[64,8192]{1,0:T(8,128)(2,1)} %all-gather.6.cloned.1.call-done, bf16[512,8192]{1,0:T(8,128)(2,1)} %param.13), kind=kOutput, calls=%fused_computation.17 | convolution fusion | flops 536870912 | bytes 9568256 | tf_op jit(solution)/shard_map/dot_general | solution.py:26
  114.4 0.0 all-to-all-done.2
  114.4 3.4 %all-to-all-start.1 = ((f32[8,8,512]{2,1,0:T(8,128)}), f32[8,8,512]{2,1,0:T(8,128)S(1)}, u32[]{:S(2)}, u32[]{:S(2)}) async-start(f32[8,8,512]{2,1,0:T(8,128)} %convolution_bitcast_fusion), calls=%async_computation.2 | async-start | bytes 262144 | tf_op jit(solution)/shard_map/all_to_all | solution.py:82
  117.8 0.0 reduce-scatter.5.cloned.1.call-start
  117.8 8.6 %fusion.10 = f32[8192,512]{0,1:T(8,128)} fusion(s32[8192]{0:T(1024)S(1)} %iota_add_fusion, s32[64]{0:T(128)S(1)} %all-reduce.4, bf16[8,8,512]{2,0,1:T(8,128)(2,1)S(1)} %all-to-all-done.2), kind=kOutput, calls=%fused_computation.15 | convolution fusion | flops 537395200 | bytes 16875776 | tf_op jit(solution)/shard_map/dot_general | solution.py:20
  126.4 0.0 all-to-all-done.1
  126.4 0.7 copy-done.2
  127.0 0.0 reduce-scatter.5.cloned.1.call-update
  127.1 14.3 %bitcast_add_fusion = f32[512,8192]{1,0:T(8,128)} fusion(f32[8192,512]{0,1:T(8,128)} %fusion.10, bf16[64,8192]{1,0:T(8,128)(2,1)S(1)} %copy-done, bf16[8,8,512]{2,1,0:T(8,128)(2,1)S(1)} %all_to_all.43), kind=kOutput, calls=%fused_computation.14 | convolution fusion | flops 541065216 | bytes 34668544 | tf_op jit(solution)/shard_map/dot_general | solution.py:20
  141.4 6.6 %reduce-scatter.5.cloned.1.call-done = f32[8,1024]{1,0:T(8,128)} async-done(((f32[8,4096]{1,0:T(8,128)}), f32[8,1024]{1,0:T(8,128)}) %reduce-scatter.5.cloned.1.call-update) | async-done | bytes 32784 | tf_op jit(solution)/shard_map/reduce_scatter | solution.py:83
  148.0 1.4 convert_element_type.12
  (23 shorter events, 0.1 us)
Async XLA Ops:
  7.2 62.7 %reduce-scatter.3.cloned.1.call-start = ((), (), s32[]{:S(2)}) async-start(), calls=%async_computation.5 | async-start | bytes 2359296 | tf_op jit(solution)/shard_map/reduce_scatter | solution.py:55
  22.8 6.4 %copy-start.1 = (bf16[8,8192]{1,0:T(8,128)(2,1)S(1)}, bf16[8,8192]{1,0:T(8,128)(2,1)}, u32[]{:S(2)}) copy-start(bf16[8,8192]{1,0:T(8,128)(2,1)} %param.12) | copy-start | bytes 393220
  22.8 6.6 %copy-start.6 = (u32[32]{0:T(128)S(1)}, u32[32]{0:T(128)}, u32[]{:S(2)}) copy-start(u32[32]{0:T(128)} %constant.69) | copy-start | bytes 388
  22.8 62.0 %copy-start.3 = (f32[8]{0:T(128)S(1)}, f32[8]{0:T(128)}, u32[]{:S(2)}) copy-start(f32[8]{0:T(128)} %param.11) | copy-start | bytes 100
  22.8 67.2 %copy-start.5 = (u32[32]{0:T(128)S(1)}, u32[32]{0:T(128)}, u32[]{:S(2)}) copy-start(u32[32]{0:T(128)} %constant.89) | copy-start | bytes 388
  22.8 68.4 %copy-start.4 = (s32[8]{0:T(128)S(1)}, s32[8]{0:T(128)}, u32[]{:S(2)}) copy-start(s32[8]{0:T(128)} %param.10) | copy-start | bytes 100
  29.2 78.2 %all-gather.6.cloned.1.call-start = ((), (), s32[]{:S(2)}) async-start(), calls=%async_computation.6 | async-start | bytes 1179648 | tf_op jit(solution)/shard_map/all_gather | solution.py:76
  86.6 27.8 %all-to-all-start.2 = ((bf16[8,8,512]{2,0,1:T(8,128)(2,1)}), bf16[8,8,512]{2,0,1:T(8,128)(2,1)S(1)}, u32[]{:S(2)}, u32[]{:S(2)}) async-start(bf16[8,8,512]{2,0,1:T(8,128)(2,1)} %bitcast.18), calls=%async_computation.4 | async-start | bytes 131072 | tf_op jit(solution)/shard_map/all_to_all | solution.py:53
  114.4 12.0 %all-to-all-start.1 = ((f32[8,8,512]{2,1,0:T(8,128)}), f32[8,8,512]{2,1,0:T(8,128)S(1)}, u32[]{:S(2)}, u32[]{:S(2)}) async-start(f32[8,8,512]{2,1,0:T(8,128)} %convolution_bitcast_fusion), calls=%async_computation.2 | async-start | bytes 262144 | tf_op jit(solution)/shard_map/all_to_all | solution.py:82
  117.8 9.3 %copy-start = (bf16[64,8192]{1,0:T(8,128)(2,1)S(1)}, bf16[64,8192]{1,0:T(8,128)(2,1)}, u32[]{:S(2)}) copy-start(bf16[64,8192]{1,0:T(8,128)(2,1)} %all-gather.6.cloned.1.call-done) | copy-start | bytes 3145732
  117.8 30.2 %reduce-scatter.5.cloned.1.call-start = ((), (), s32[]{:S(2)}) async-start(), calls=%async_computation.7 | async-start | bytes 163840 | tf_op jit(solution)/shard_map/reduce_scatter | solution.py:83
  126.4 0.7 copy-start.2
Sparse Core Ops, SparseCore 0:
  29.3 40.5 reduce-scatter.2
  86.7 20.5 all-gather.5
  127.2 20.7 reduce-scatter.4
